TPU v7x, 32 devices: a whole 2x2x4 slice. The times are simulated.
32 devices in a mesh: row: 8 (over z, y), col: 4 (over x, core).
Axes of the slice: x: 2, y: 2, z: 4, core: 2. Of those that a mesh axis runs over, the one named last changes fastest.
Arguments:
- embeddings: float32 [32768, 2048], P('row', 'col'), may hold values from -2.5 to 2.5
- selected: int32 [512], replicated, may hold values from 0 to 32767, as said below
Outputs:
- sample_share: float32 [32768], P(('row', 'col'))
- log_gain: float32 [32768], P(('row', 'col'))
- logdet_mean: float32 [], replicated
Inputs may be any that keep to these rules, and one draw needn't show every extreme that they name: `selected`: 512 distinct item indices.
All inputs are finite; a program needn't handle non-finite values.
Results may differ from a plain program's by a relative error of at most 0.0003.
Values sent between devices are 32-bit elements; how exact they have to be, the bound alone decides.
No kernel may reach another device: no remote copies, remote signals or barrier semaphores. Data moves between devices by JAX's collectives and lax.ppermute only.
A program may use at most 64 MiB of HBM per device.

v0:
```python
import jax
import jax.numpy as jnp
from jax import lax
from jax.sharding import PartitionSpec as P

K = 512


def local(embeddings, selected):
    rows_here = embeddings.shape[0]
    my_index = lax.axis_index("row")
    first_row = my_index * rows_here
    offsets = selected - first_row
    inside = (offsets >= 0) & (offsets < rows_here)
    picked = jnp.take(embeddings, jnp.clip(offsets, 0, rows_here - 1), axis=0)
    picked = jnp.where(inside[:, None], picked, jnp.zeros_like(picked))
    chosen = lax.psum(picked, "row")
    partial_value = jnp.dot(chosen, chosen.T, precision=lax.Precision.HIGHEST)
    kernel = lax.psum(partial_value, "col")
    kernel = kernel + jnp.eye(K, dtype=jnp.float32)
    factor = jnp.linalg.cholesky(kernel)
    logdet_mean = 2.0 * jnp.sum(jnp.log(jnp.diagonal(factor))) / K
    whitened = jax.scipy.linalg.solve_triangular(factor, chosen, lower=True)
    whitened_full = lax.all_gather(whitened, "col", axis=1, tiled=True)
    regrouped = lax.all_to_all(embeddings, "col", split_axis=0, concat_axis=1, tiled=True)
    coordinates = jnp.dot(regrouped, whitened_full.T, precision=lax.Precision.HIGHEST)
    gain = jnp.sum(regrouped * regrouped, axis=1) + 1.0 - jnp.sum(coordinates * coordinates, axis=1)
    item_count = rows_here * lax.axis_size("row")
    grand_total = lax.psum(jnp.sum(gain), ("row", "col"))
    sample_share = gain * (item_count / grand_total)
    return (sample_share, jnp.log(gain), logdet_mean)


def solution(mesh):
    return jax.shard_map(
        local,
        mesh=mesh,
        in_specs=(P("row", "col"), P()),
        out_specs=(P(("row", "col")), P(("row", "col")), P()),
        check_vma=False,
    )
```

profile of v0, /device:TPU:0, one launch (start us, length us, event | category | flops | bytes accessed | tf_op | source)
XLA Modules:
  0.0 404.0 jit_solution(5842791233570516075)
XLA Ops:
  7.9 5.4 %gather_fusion = f32[512,512]{1,0:T(8,128)S(1)} fusion(f32[4096,512]{1,0:T(8,128)} %param.2, s32[1024]{0:T(1024)S(1)} %pad_clamp_fusion), kind=kCustom, calls=%fused_computation | custom fusion | bytes 2099200 | tf_op jit(solution)/shard_map/jit(_take)/gather | solution.py:15
  14.6 81.2 %all-reduce.4.cloned.1.call-done = f32[512,512]{1,0:T(8,128)} async-done(((f32[512,512]{1,0:T(8,128)}), f32[512,512]{1,0:T(8,128)}) %all-reduce.4.cloned.1.call-update) | async-done | bytes 1048592 | tf_op jit(solution)/shard_map/psum | solution.py:17
  95.8 4.6 %fusion.34 = f32[512,512]{0,1:T(8,128)} fusion(f32[512,512]{1,0:T(8,128)} %all-reduce.4.cloned.1.call-done), kind=kOutput, calls=%fused_computation.85 | convolution fusion | flops 1610612736 | bytes 2097152 | tf_op jit(solution)/shard_map/dot_general | solution.py:18
  100.4 5.7 %all-to-all-start = ((f32[4,1024,512]{2,1,0:T(8,128)}), f32[4,1024,512]{2,1,0:T(8,128)}, u32[]{:S(2)}, u32[]{:S(2)}) async-start(f32[4,1024,512]{2,1,0:T(8,128)} %bitcast.58), calls=%async_computation | async-start | bytes 16777216 | tf_op jit(solution)/shard_map/all_to_all | solution.py:25
  106.4 45.0 %all-reduce.6.cloned.1.call-done = f32[512,512]{0,1:T(8,128)} async-done(((f32[512,512]{0,1:T(8,128)}), f32[512,512]{0,1:T(8,128)}) %all-reduce.6.cloned.1.call-update) | async-done | bytes 1048592 | tf_op jit(solution)/shard_map/psum | solution.py:19
  151.5 1.3 convert_add_fusion
  153.1 1.4 fusion
  155.6 11.7 %cholesky.102 = f32[128,128]{1,0:T(8,128)S(1)} custom-call(f32[128,128]{1,0:T(8,128)S(1)} %cholesky.260), custom_call_target="Cholesky" | custom-call | tf_op jit(solution)/shard_map/jit(cholesky)/cholesky | solution.py:21
  167.3 9.8 %custom-call.31 = f32[1,128,128]{1,2,0:T(8,128)S(1)} custom-call(f32[1,128,128]{2,1,0:T(8,128)S(1)} %get-tuple-element.34), custom_call_target="InvertDiagBlocksLowerTriangular" | custom-call | tf_op jit(solution)/shard_map/jit(cholesky)/cholesky | solution.py:21
  177.3 1.2 constant_dynamic-update-slice_fusion.3
  178.5 1.3 convolution_subtract_fusion.3
  179.8 11.7 %cholesky.213 = f32[128,128]{1,0:T(8,128)S(1)} custom-call(f32[128,128]{1,0:T(8,128)S(1)} %cholesky.264), custom_call_target="Cholesky" | custom-call | tf_op jit(solution)/shard_map/jit(cholesky)/cholesky | solution.py:21
  191.6 10.3 %custom-call.32 = f32[1,128,128]{1,2,0:T(8,128)S(1)} custom-call(f32[1,128,128]{2,1,0:T(8,128)S(1)} %get-tuple-element.31), custom_call_target="InvertDiagBlocksLowerTriangular" | custom-call | tf_op jit(solution)/shard_map/jit(cholesky)/cholesky | solution.py:21
  202.1 1.3 convolution_subtract_fusion.4
  203.4 11.7 %cholesky.234 = f32[128,128]{1,0:T(8,128)S(1)} custom-call(f32[128,128]{1,0:T(8,128)S(1)} %cholesky.269), custom_call_target="Cholesky" | custom-call | tf_op jit(solution)/shard_map/jit(cholesky)/cholesky | solution.py:21
  215.9 9.8 %custom-call.33 = f32[1,128,128]{1,2,0:T(8,128)S(1)} custom-call(f32[1,128,128]{2,1,0:T(8,128)S(1)} %get-tuple-element.28), custom_call_target="InvertDiagBlocksLowerTriangular" | custom-call | tf_op jit(solution)/shard_map/jit(cholesky)/cholesky | solution.py:21
  227.1 11.7 %cholesky.251 = f32[128,128]{1,0:T(8,128)S(1)} custom-call(f32[128,128]{1,0:T(8,128)S(1)} %convolution_subtract_fusion.5), custom_call_target="Cholesky" | custom-call | tf_op jit(solution)/shard_map/jit(cholesky)/cholesky | solution.py:21
  243.0 1.2 fusion.1
  244.2 11.6 %while.1 = (s32[]{:T(128)}, f32[512,512]{1,0:T(8,128)}, s32[4,2]{0,1:T(2,128)S(1)}, f32[4,128,128]{2,1,0:T(8,128)S(1)}, s32[]{:T(128)}) while((s32[]{:T(128)}, f32[512,512]{1,0:T(8,128)}, s32[4,2]{0,1:T(2,128)S(1)}, f32[4,128,128]{2,1,0:T(8,128)S(1)}, s32[]{:T(128)}) %tuple.35), condition=%wide.while_cond, body=%wide.while_body.sunk | while | flops 2 | bytes 131189 | solution.py:23
  244.8 2.3 bitcast_dynamic-update-slice_fusion.2
  247.7 2.3 bitcast_dynamic-update-slice_fusion.2
  250.6 2.3 bitcast_dynamic-update-slice_fusion.2
  253.6 2.2 bitcast_dynamic-update-slice_fusion.2
  255.8 39.3 %custom-call.34 = f32[4,128,128]{1,2,0:T(8,128)S(1)} custom-call(f32[4,128,128]{2,1,0:T(8,128)S(1)} %get-tuple-element.10), custom_call_target="InvertDiagBlocksLowerTriangular" | custom-call | tf_op jit(solution)/shard_map/jit(_solve_triangular)/triangular_solve | solution.py:23
  297.2 1.3 convolution_subtract_fusion
  299.0 1.6 convolution_subtract_fusion.2
  302.0 4.5 %gather_fusion.1 = f32[512]{0:T(512)S(1)} fusion(f32[512,512]{1,0:T(8,128)S(1)} %get-tuple-element.20, s32[512]{0:T(512)S(1)} %bitcast.57), kind=kCustom, calls=%fused_computation.1 | custom fusion | bytes 8192 | tf_op jit(solution)/shard_map/jit(diagonal)/cond/branch_0_fun/gather | solution.py:22
  307.2 9.3 %copy.11 = f32[1024,4,512]{0,2,1:T(8,128)} copy(f32[1024,4,512]{2,0,1:T(8,128)} %bitcast.1) | data formatting | bytes 16777216 | tf_op jit(solution)/shard_map/all_to_all | solution.py:25
  316.4 4.0 multiply_reduce_fusion
  320.4 16.2 %all-gather.2.cloned.1.call-done = f32[512,2048]{1,0:T(8,128)} async-done(((f32[512,512]{1,0:T(8,128)}), f32[512,2048]{1,0:T(8,128)}) %all-gather.2.cloned.1.call-update) | async-done | bytes 4194320 | tf_op jit(solution)/shard_map/all_gather | solution.py:24
  336.6 17.3 %multiply_reduce_fusion.1 = f32[1024]{0:T(1024)S(1)} fusion(f32[512,2048]{1,0:T(8,128)} %all-gather.2.cloned.1.call-done, f32[1024,2048]{0,1:T(8,128)} %bitcast.59), kind=kOutput, calls=%fused_computation.5 | convolution fusion | flops 12885949440 | bytes 12587008 | tf_op jit(solution)/shard_map/dot_general | solution.py:26
  355.2 39.6 %psum.23 = f32[]{:T(128)} all-reduce(f32[]{:T(128)} %fusion.32), channel_id=1, replica_groups=mesh['row'=8,'col'=4] {'row','col'}, use_global_device_ids=true, to_apply=%region_13.14 | all-reduce | flops 1 | bytes 8 | tf_op jit(solution)/shard_map/psum | solution.py:29
  (50 shorter events, 16.0 us)
Async XLA Ops:
  7.2 88.6 %all-reduce.4.cloned.1.call-start = ((), (), s32[]{:S(2)}) async-start(), calls=%async_computation.1 | async-start | bytes 2097152 | tf_op jit(solution)/shard_map/psum | solution.py:17
  14.6 136.9 %all-reduce.6.cloned.1.call-start = ((), (), s32[]{:S(2)}) async-start(), calls=%async_computation.2 | async-start | bytes 2097152 | tf_op jit(solution)/shard_map/psum | solution.py:19
  100.4 206.8 %all-to-all-start = ((f32[4,1024,512]{2,1,0:T(8,128)}), f32[4,1024,512]{2,1,0:T(8,128)}, u32[]{:S(2)}, u32[]{:S(2)}) async-start(f32[4,1024,512]{2,1,0:T(8,128)} %bitcast.58), calls=%async_computation | async-start | bytes 16777216 | tf_op jit(solution)/shard_map/all_to_all | solution.py:25
  106.1 189.1 %copy-start = (f32[512,512]{1,0:T(8,128)S(1)}, f32[512,512]{1,0:T(8,128)}, u32[]{:S(2)}) copy-start(f32[512,512]{1,0:T(8,128)} %all-reduce.4.cloned.1.call-done) | copy-start | bytes 3145732
  106.1 230.6 %all-gather.2.cloned.1.call-start = ((), (), s32[]{:S(2)}) async-start(), calls=%async_computation.3 | async-start | bytes 5242880 | tf_op jit(solution)/shard_map/all_gather | solution.py:24
  154.6 1.0 copy-start.1
Sparse Core Ops, SparseCore 0:
  14.7 81.0 all-reduce.3
  100.5 50.9 all-reduce.5
  302.1 34.4 all-gather.1
where the time goes:
time: 408 us; the launch traced here: 404 us
  waiting for transfers between devices  142 us (35%)
  other arithmetic  131 us (32%)
  blocking collectives  39.6 us (10%)
  matrix products  33.1 us (8%)
  local copies, waits for them, and re-layouts  32.1 us (8%)
  between operations  19.3 us (5%)
  starting transfers between devices  6.08 us (1%)
    psum x1, waiting for transfers between devices, local(): chosen = lax.psum(picked, 'row')  81.2 us
    another operation x14, other arithmetic, local(): factor = jnp.linalg.cholesky(kernel)  79.1 us
    psum x1, waiting for transfers between devices, local(): kernel = lax.psum(partial_value, 'col')  45 us
    another operation x4, other arithmetic, local(): whitened = jax.scipy.linalg.solve_triangular(factor, chosen, lower=True)  41.6 us
    psum x1, blocking collectives, local(): grand_total = lax.psum(jnp.sum(gain), ('row', 'col'))  39.6 us
    dot_general x1, matrix products, local(): jnp.dot(regrouped, whitened_full.T, precision=lax.Precision.HIGHEST)  17.3 us
    all_gather x1, waiting for transfers between devices, local(): whitened_full = lax.all_gather(whitened, 'col', axis=1, tiled=True)  16.2 us
    another operation x12, local copies, waits for them, and re-layouts  11.5 us
  transfers between devices with their start and end apart: 4, of which 3 were waited for; matrix products, arithmetic and copies ran while one was open for 41% of the time, Pallas kernels for 0%

commit v1 on v0

--- a/solution.py
+++ b/solution.py
@@ -16,7 +16,7 @@
     picked = jnp.where(inside[:, None], picked, jnp.zeros_like(picked))
     chosen = lax.psum(picked, "row")
     partial_value = jnp.dot(chosen, chosen.T, precision=lax.Precision.HIGHEST)
-    kernel = lax.psum(partial_value, "col")
+    kernel = jnp.sum(lax.all_gather(partial_value, "col"), axis=0)
     kernel = kernel + jnp.eye(K, dtype=jnp.float32)
     factor = jnp.linalg.cholesky(kernel)
     logdet_mean = 2.0 * jnp.sum(jnp.log(jnp.diagonal(factor))) / K

time: 408 us -> 414 us (1.015)
  waiting for transfers between devices: 142 us -> 148 us
    all_gather x0 -> x1, waiting for transfers between devices: none -> 50.7 us  [local(): kernel = jnp.sum(lax.all_gather(partial_value, 'col'), axis=0)]
    psum x1 -> x0, waiting for transfers between devices: 45 us -> none  [local(): kernel = lax.psum(partial_value, 'col')]
  transfers between devices with their start and end apart: 4 -> 4, of which waited for: 3 -> 3; matrix products, arithmetic and copies ran while one was open for 41% -> 40% of each run, Pallas kernels for 0% -> 0%
where the time goes in v1:
time: 414 us; the launch traced here: 410 us
  waiting for transfers between devices  148 us (36%)
  other arithmetic  132 us (32%)
  blocking collectives  39.6 us (10%)
  matrix products  33.1 us (8%)
  local copies, waits for them, and re-layouts  31.8 us (8%)
  between operations  19.2 us (5%)
  starting transfers between devices  6.08 us (1%)
    psum x1, waiting for transfers between devices, local(): chosen = lax.psum(picked, 'row')  81.2 us
    another operation x14, other arithmetic, local(): factor = jnp.linalg.cholesky(kernel)  79 us
    all_gather x1, waiting for transfers between devices, local(): kernel = jnp.sum(lax.all_gather(partial_value, 'col'), axis=0)  50.7 us
    another operation x4, other arithmetic, local(): whitened = jax.scipy.linalg.solve_triangular(factor, chosen, lower=True)  41.7 us
    psum x1, blocking collectives, local(): grand_total = lax.psum(jnp.sum(gain), ('row', 'col'))  39.6 us
    dot_general x1, matrix products, local(): jnp.dot(regrouped, whitened_full.T, precision=lax.Precision.HIGHEST)  17.3 us
    all_gather x1, waiting for transfers between devices, local(): whitened_full = lax.all_gather(whitened, 'col', axis=1, tiled=True)  16.4 us
    another operation x12, local copies, waits for them, and re-layouts  11.5 us
  transfers between devices with their start and end apart: 4, of which 3 were waited for; matrix products, arithmetic and copies ran while one was open for 40% of the time, Pallas kernels for 0%

profile of v1, /device:TPU:0, one launch (start us, length us, event | category | flops | bytes accessed | tf_op | source)
XLA Modules:
  0.0 409.8 jit_solution(17591757986898578238)
XLA Ops:
  7.9 5.4 %gather_fusion = f32[512,512]{1,0:T(8,128)S(1)} fusion(f32[4096,512]{1,0:T(8,128)} %param.2, s32[1024]{0:T(1024)S(1)} %pad_clamp_fusion), kind=kCustom, calls=%fused_computation | custom fusion | bytes 2099200 | tf_op jit(solution)/shard_map/jit(_take)/gather | solution.py:15
  14.6 81.2 %all-reduce.3.cloned.1.call-done = f32[512,512]{1,0:T(8,128)} async-done(((f32[512,512]{1,0:T(8,128)}), f32[512,512]{1,0:T(8,128)}) %all-reduce.3.cloned.1.call-update) | async-done | bytes 1048592 | tf_op jit(solution)/shard_map/psum | solution.py:17
  95.8 4.5 %fusion.35 = f32[512,512]{1,0:T(8,128)} fusion(f32[512,512]{1,0:T(8,128)} %all-reduce.3.cloned.1.call-done), kind=kOutput, calls=%fused_computation.86 | convolution fusion | flops 1610612736 | bytes 2097152 | tf_op jit(solution)/shard_map/dot_general | solution.py:18
  100.3 5.7 %all-to-all-start = ((f32[4,1024,512]{2,1,0:T(8,128)}), f32[4,1024,512]{2,1,0:T(8,128)}, u32[]{:S(2)}, u32[]{:S(2)}) async-start(f32[4,1024,512]{2,1,0:T(8,128)} %bitcast.61), calls=%async_computation | async-start | bytes 16777216 | tf_op jit(solution)/shard_map/all_to_all | solution.py:25
  106.3 50.7 %all-gather.6.cloned.1.call-done = f32[2048,512]{1,0:T(8,128)} async-done(((f32[512,512]{1,0:T(8,128)}), f32[2048,512]{1,0:T(8,128)}) %all-gather.6.cloned.1.call-update) | async-done | bytes 4194320 | tf_op jit(solution)/shard_map/all_gather | solution.py:19
  157.1 2.8 reduce_sum.48
  161.5 11.7 %cholesky.102 = f32[128,128]{1,0:T(8,128)S(1)} custom-call(f32[128,128]{1,0:T(8,128)S(1)} %cholesky.260), custom_call_target="Cholesky" | custom-call | tf_op jit(solution)/shard_map/jit(cholesky)/cholesky | solution.py:21
  173.4 9.8 %custom-call.31 = f32[1,128,128]{1,2,0:T(8,128)S(1)} custom-call(f32[1,128,128]{2,1,0:T(8,128)S(1)} %get-tuple-element.34), custom_call_target="InvertDiagBlocksLowerTriangular" | custom-call | tf_op jit(solution)/shard_map/jit(cholesky)/cholesky | solution.py:21
  183.2 1.2 constant_dynamic-update-slice_fusion.3
  184.5 1.3 convolution_subtract_fusion.3
  185.7 11.7 %cholesky.213 = f32[128,128]{1,0:T(8,128)S(1)} custom-call(f32[128,128]{1,0:T(8,128)S(1)} %cholesky.264), custom_call_target="Cholesky" | custom-call | tf_op jit(solution)/shard_map/jit(cholesky)/cholesky | solution.py:21
  197.5 10.3 %custom-call.32 = f32[1,128,128]{1,2,0:T(8,128)S(1)} custom-call(f32[1,128,128]{2,1,0:T(8,128)S(1)} %get-tuple-element.31), custom_call_target="InvertDiagBlocksLowerTriangular" | custom-call | tf_op jit(solution)/shard_map/jit(cholesky)/cholesky | solution.py:21
  208.1 1.3 convolution_subtract_fusion.4
  209.4 11.7 %cholesky.234 = f32[128,128]{1,0:T(8,128)S(1)} custom-call(f32[128,128]{1,0:T(8,128)S(1)} %cholesky.269), custom_call_target="Cholesky" | custom-call | tf_op jit(solution)/shard_map/jit(cholesky)/cholesky | solution.py:21
  221.8 9.8 %custom-call.33 = f32[1,128,128]{1,2,0:T(8,128)S(1)} custom-call(f32[1,128,128]{2,1,0:T(8,128)S(1)} %get-tuple-element.28), custom_call_target="InvertDiagBlocksLowerTriangular" | custom-call | tf_op jit(solution)/shard_map/jit(cholesky)/cholesky | solution.py:21
  231.8 1.2 convolution_subtract_fusion.5
  233.1 11.9 %cholesky.251 = f32[128,128]{1,0:T(8,128)S(1)} custom-call(f32[128,128]{1,0:T(8,128)S(1)} %convolution_subtract_fusion.5), custom_call_target="Cholesky" | custom-call | tf_op jit(solution)/shard_map/jit(cholesky)/cholesky | solution.py:21
  248.7 1.3 fusion.2
  250.1 11.6 %while.1 = (s32[]{:T(128)}, f32[512,512]{1,0:T(8,128)}, s32[4,2]{0,1:T(2,128)S(1)}, f32[4,128,128]{2,1,0:T(8,128)S(1)}, s32[]{:T(128)}) while((s32[]{:T(128)}, f32[512,512]{1,0:T(8,128)}, s32[4,2]{0,1:T(2,128)S(1)}, f32[4,128,128]{2,1,0:T(8,128)S(1)}, s32[]{:T(128)}) %tuple.35), condition=%wide.while_cond, body=%wide.while_body.sunk | while | flops 2 | bytes 131189 | solution.py:23
  250.7 2.3 bitcast_dynamic-update-slice_fusion.2
  253.6 2.3 bitcast_dynamic-update-slice_fusion.2
  256.5 2.3 bitcast_dynamic-update-slice_fusion.2
  259.4 2.2 bitcast_dynamic-update-slice_fusion.2
  261.6 39.3 %custom-call.34 = f32[4,128,128]{1,2,0:T(8,128)S(1)} custom-call(f32[4,128,128]{2,1,0:T(8,128)S(1)} %get-tuple-element.10), custom_call_target="InvertDiagBlocksLowerTriangular" | custom-call | tf_op jit(solution)/shard_map/jit(_solve_triangular)/triangular_solve | solution.py:23
  303.0 1.3 convolution_subtract_fusion
  304.8 1.6 convolution_subtract_fusion.2
  307.9 8.8 %copy.10 = f32[1024,4,512]{0,2,1:T(8,128)} copy(f32[1024,4,512]{2,0,1:T(8,128)} %bitcast.1) | data formatting | bytes 16777216 | tf_op jit(solution)/shard_map/all_to_all | solution.py:25
  316.7 4.2 %multiply_reduce_fusion = f32[1024]{0:T(1024)S(1)} fusion(f32[4,1024,512]{2,1,0:T(8,128)} %all-to-all-done), kind=kLoop, calls=%fused_computation.4 | loop fusion | flops 4193280 | bytes 8392704 | tf_op jit(solution)/shard_map/reduce_sum | solution.py:27
  320.9 4.5 %gather_fusion.1 = f32[512]{0:T(512)S(1)} fusion(f32[512,512]{1,0:T(8,128)S(1)} %get-tuple-element.20, s32[512]{0:T(512)S(1)} %bitcast.60), kind=kCustom, calls=%fused_computation.1 | custom fusion | bytes 8192 | tf_op jit(solution)/shard_map/jit(diagonal)/cond/branch_0_fun/gather | solution.py:22
  326.0 16.4 %all-gather.4.cloned.1.call-done = f32[512,2048]{1,0:T(8,128)} async-done(((f32[512,512]{1,0:T(8,128)}), f32[512,2048]{1,0:T(8,128)}) %all-gather.4.cloned.1.call-update) | async-done | bytes 4194320 | tf_op jit(solution)/shard_map/all_gather | solution.py:24
  342.5 17.3 %multiply_reduce_fusion.1 = f32[1024]{0:T(1024)S(1)} fusion(f32[512,2048]{1,0:T(8,128)} %all-gather.4.cloned.1.call-done, f32[1024,2048]{0,1:T(8,128)} %bitcast.62), kind=kOutput, calls=%fused_computation.5 | convolution fusion | flops 12885949440 | bytes 12587008 | tf_op jit(solution)/shard_map/dot_general | solution.py:26
  361.1 39.6 %psum.15 = f32[]{:T(128)} all-reduce(f32[]{:T(128)} %fusion.33), channel_id=1, replica_groups=mesh['row'=8,'col'=4] {'row','col'}, use_global_device_ids=true, to_apply=%region_13.14 | all-reduce | flops 1 | bytes 8 | tf_op jit(solution)/shard_map/psum | solution.py:29
  (50 shorter events, 14.8 us)
Async XLA Ops:
  7.2 88.6 %all-reduce.3.cloned.1.call-start = ((), (), s32[]{:S(2)}) async-start(), calls=%async_computation.1 | async-start | bytes 2097152 | tf_op jit(solution)/shard_map/psum | solution.py:17
  14.6 142.5 %all-gather.6.cloned.1.call-start = ((), (), s32[]{:S(2)}) async-start(), calls=%async_computation.3 | async-start | bytes 5242880 | tf_op jit(solution)/shard_map/all_gather | solution.py:19
  100.3 207.6 %all-to-all-start = ((f32[4,1024,512]{2,1,0:T(8,128)}), f32[4,1024,512]{2,1,0:T(8,128)}, u32[]{:S(2)}, u32[]{:S(2)}) async-start(f32[4,1024,512]{2,1,0:T(8,128)} %bitcast.61), calls=%async_computation | async-start | bytes 16777216 | tf_op jit(solution)/shard_map/all_to_all | solution.py:25
  106.0 236.5 %all-gather.4.cloned.1.call-start = ((), (), s32[]{:S(2)}) async-start(), calls=%async_computation.2 | async-start | bytes 5242880 | tf_op jit(solution)/shard_map/all_gather | solution.py:24
  159.9 141.1 %copy-start = (f32[512,512]{1,0:T(8,128)S(1)}, f32[512,512]{1,0:T(8,128)}, u32[]{:S(2)}) copy-start(f32[512,512]{1,0:T(8,128)} %all-reduce.3.cloned.1.call-done) | copy-start | bytes 3145732
  160.4 1.1 copy-start.1
Sparse Core Ops, SparseCore 0:
  14.7 81.0 all-reduce.2
  100.4 56.6 all-gather.5
  308.0 34.4 all-gather.3
